TPU v7x, 32 devices: a whole 2x2x4 slice. The times are simulated.
32 devices in a mesh: fsdp: 8 (over z, core), head: 4 (over y, x).
Axes of the slice: x: 2, y: 2, z: 4, core: 2. Of those that a mesh axis runs over, the one named last changes fastest.
Arguments:
- probe_compressed: bfloat16 [2, 32, 1536], P(None, 'fsdp'), may hold values from -6 to 6
- w_uq: bfloat16 [1536, 16384], P('fsdp', 'head'), may hold values from -0.15625 to 0.15625
- w_qr: bfloat16 [1536, 8192], P('fsdp', 'head'), may hold values from -0.15625 to 0.15625
- w_uk: bfloat16 [512, 16384], P('fsdp', 'head'), may hold values from -0.25 to 0.25
- w_uv: bfloat16 [512, 16384], P('fsdp', 'head'), may hold values from -1.5 to 1.5
- cache: bfloat16 [32, 1024, 576], P(('fsdp', 'head')), may hold values from -136 to 136
- new_kv: bfloat16 [2, 32, 576], P(None, ('fsdp', 'head')), may hold values from -6 to 6
- lengths: int32 [32], P(('fsdp', 'head')), may hold values from 1 to 1024
Outputs:
- values: bfloat16 [2, 32, 16384], P(None, 'fsdp', 'head')
All inputs are finite; a program needn't handle non-finite values.
Results may differ from a plain program's by a relative error of at most 0.035.
Values may be sent and summed in bfloat16 or wider, within the bound.
A program may use at most 64 MiB of HBM per device.

v0:
```python
import jax
import jax.numpy as jnp
from jax import lax
from jax.sharding import PartitionSpec as P

NOPE = 128
R = 64
VDIM = 128


def rotate(rope_part, position):
    half = rope_part.shape[-1] // 2
    freqs = 10000.0 ** (-(jnp.arange(half, dtype=jnp.float32) * 2.0 / (2 * half)))
    angle = position[..., None] * freqs
    first = rope_part[..., :half]
    second = rope_part[..., half:]
    cosine_table = jnp.cos(angle)
    sine = jnp.sin(angle)
    return jnp.concatenate(
        [first * cosine_table - second * sine, first * sine + second * cosine_table], axis=-1
    )


def attend(query, keys, fresh, extent):
    steps = query.shape[0]
    heads = query.shape[1]
    width = keys.shape[1]
    latent_width = width - R
    position = (extent + jnp.arange(steps, dtype=jnp.int32)).astype(jnp.float32)
    rotated = rotate(query[:, :, latent_width:].astype(jnp.float32), position[:, None])
    joined = jnp.concatenate([query[:, :, :latent_width], rotated.astype(jnp.bfloat16)], axis=2)
    joined = joined.reshape(steps * heads, width)
    factor = (NOPE + R) ** (-0.5)
    older = jnp.dot(joined, keys.T, preferred_element_type=jnp.float32) * factor
    valid = jnp.arange(keys.shape[0], dtype=jnp.int32) < extent
    older = jnp.where(valid[None, :], older, -1e30)
    newer = jnp.dot(joined, fresh.T, preferred_element_type=jnp.float32) * factor
    order = jnp.arange(steps, dtype=jnp.int32)
    allowed = jnp.repeat(order[None, :] <= order[:, None], heads, axis=0)
    newer = jnp.where(allowed, newer, -1e30)
    highest = jnp.maximum(jnp.max(older, axis=1), jnp.max(newer, axis=1))
    weight_old = jnp.exp(older - highest[:, None])
    weight_new = jnp.exp(newer - highest[:, None])
    total = jnp.sum(weight_old, axis=1) + jnp.sum(weight_new, axis=1)
    mixed = jnp.dot(
        weight_old.astype(jnp.bfloat16), keys[:, :latent_width], preferred_element_type=jnp.float32
    )
    mixed = mixed + jnp.dot(
        weight_new.astype(jnp.bfloat16), fresh[:, :latent_width], preferred_element_type=jnp.float32
    )
    return (mixed / total[:, None]).astype(jnp.bfloat16).reshape(steps, heads, latent_width)


def per_device(probe_compressed, w_uq, w_qr, w_uk, w_uv, cache, new_kv, lengths):
    heads = w_uk.shape[1] // NOPE
    steps, group, rank = probe_compressed.shape
    flattened = probe_compressed.reshape(steps * group, rank)
    key_up, value_up, rotary_up_weight = (
        lax.all_gather(w_uk, "fsdp", axis=0, tiled=True),
        lax.all_gather(w_uv, "fsdp", axis=0, tiled=True),
        lax.all_gather(w_qr, "fsdp", axis=0, tiled=True),
    )
    key_heads = key_up.reshape(key_up.shape[0], heads, NOPE)
    slab = lax.all_gather(w_uq, "fsdp", axis=0, tiled=True)
    count = slab.shape[0]
    slab_heads = slab.reshape(count, heads, NOPE)
    absorbed = jnp.einsum("rhn,chn->hrc", slab_heads, key_heads, preferred_element_type=jnp.float32)
    absorbed = absorbed.astype(jnp.bfloat16)
    summed = jnp.einsum("qr,hrc->qhc", flattened, absorbed, preferred_element_type=jnp.float32)
    latent = summed.astype(jnp.bfloat16)
    latent_rank = key_up.shape[0]
    rope_query = jnp.dot(flattened, rotary_up_weight, preferred_element_type=jnp.float32).astype(
        jnp.bfloat16
    )
    rope_query = rope_query.reshape(steps * group, heads, R)
    query_matrix = jnp.concatenate([latent, rope_query], axis=2).reshape(
        steps, group, heads, latent_rank + R
    )
    row_queries = lax.all_to_all(query_matrix, "head", split_axis=1, concat_axis=2, tiled=True)
    mixed = jax.vmap(attend, in_axes=(1, 0, 1, 0), out_axes=1)(row_queries, cache, new_kv, lengths)
    combined_across_heads = lax.all_to_all(mixed, "head", split_axis=2, concat_axis=1, tiled=True)
    value_heads = value_up.reshape(latent_rank, heads, VDIM)
    attention_output = jnp.einsum(
        "sghc,chv->sghv", combined_across_heads, value_heads, preferred_element_type=jnp.float32
    )
    return attention_output.astype(jnp.bfloat16).reshape(steps, group, heads * VDIM)


def solution(mesh):
    in_specs = (
        P(None, "fsdp", None),
        P("fsdp", "head"),
        P("fsdp", "head"),
        P("fsdp", "head"),
        P("fsdp", "head"),
        P(("fsdp", "head"), None, None),
        P(None, ("fsdp", "head"), None),
        P(("fsdp", "head")),
    )
    out_specs = P(None, "fsdp", "head")
    return jax.shard_map(
        per_device, mesh=mesh, in_specs=in_specs, out_specs=out_specs, check_vma=False
    )
```

profile of v0, /device:TPU:0, one launch (start us, length us, event | category | flops | bytes accessed | tf_op | source)
XLA Modules:
  0.0 317.3 jit_solution(7329103824131219644)
XLA Ops:
  6.5 0.7 all-gather.7.cloned.1.call-update
  7.3 0.7 all-gather.9.cloned.1.call-update
  8.1 0.7 all-gather.5.cloned.1.call-update
  8.8 0.5 all-gather.11.cloned.1.call-update
  9.3 0.8 reshape.301
  10.1 0.8 reshape.292
  11.6 46.9 %all-gather.7.cloned.1.call-done = bf16[512,4096]{1,0:T(8,128)(2,1)} async-done(((bf16[64,4096]{1,0:T(8,128)(2,1)}), bf16[512,4096]{1,0:T(8,128)(2,1)}) %all-gather.7.cloned.1.call-update) | async-done | bytes 4194320 | tf_op jit(solution)/shard_map/all_gather | solution.py:59
  58.6 6.5 %copy.38 = bf16[512,4096]{0,1:T(8,128)(2,1)} copy(bf16[512,4096]{1,0:T(8,128)(2,1)} %all-gather.7.cloned.1.call-done) | data formatting | bytes 8388608 | tf_op jit(solution)/shard_map/all_gather | solution.py:59
  65.0 58.7 %all-gather.9.cloned.1.call-done = bf16[1536,2048]{1,0:T(8,128)(2,1)} async-done(((bf16[192,2048]{1,0:T(8,128)(2,1)}), bf16[1536,2048]{1,0:T(8,128)(2,1)}) %all-gather.9.cloned.1.call-update) | async-done | bytes 6291472 | tf_op jit(solution)/shard_map/all_gather | solution.py:61
  123.7 3.7 %convolution_convert_fusion = bf16[8,2048]{1,0:T(8,128)(2,1)S(1)} fusion(bf16[8,1536]{1,0:T(8,128)(2,1)S(1)} %reshape.292, bf16[1536,2048]{1,0:T(8,128)(2,1)} %all-gather.9.cloned.1.call-done), kind=kOutput, calls=%fused_computation.3 | convolution fusion | flops 50348032 | bytes 6348800 | tf_op jit(solution)/shard_map/dot_general | solution.py:72
  127.6 113.2 %all-gather.5.cloned.1.call-done = bf16[1536,4096]{1,0:T(8,128)(2,1)} async-done(((bf16[192,4096]{1,0:T(8,128)(2,1)}), bf16[1536,4096]{1,0:T(8,128)(2,1)}) %all-gather.5.cloned.1.call-update) | async-done | bytes 12582928 | tf_op jit(solution)/shard_map/all_gather | solution.py:64
  240.8 16.7 %copy.37 = bf16[1536,4096]{0,1:T(8,128)(2,1)} copy(bf16[1536,4096]{1,0:T(8,128)(2,1)} %all-gather.5.cloned.1.call-done) | data formatting | bytes 25165824 | tf_op jit(solution)/shard_map/all_gather | solution.py:64
  257.5 24.9 %fusion.11 = bf16[8,32,512]{2,0,1:T(8,128)(2,1)S(1)} fusion(bf16[8,1536,1]{1,0,2:T(8,128)(2,1)S(1)} %reshape.301, bf16[1536,32,128]{0,2,1:T(8,128)(2,1)} %bitcast.89, bf16[512,32,128]{0,2,1:T(8,128)(2,1)} %bitcast.90), kind=kOutput, calls=%fused_computation.11 | convolution fusion | flops 6870401024 | bytes 17063936 | tf_op jit(solution)/shard_map/qr,hrc->qhc/dot_general | solution.py:69
  282.6 0.8 pad_maximum_fusion
  283.4 3.7 %all-to-all-start = ((bf16[2,4,32,576]{3,2,0,1:T(8,128)(2,1)}), bf16[2,4,32,576]{3,2,0,1:T(8,128)(2,1)S(1)}, u32[]{:S(2)}, u32[]{:S(2)}) async-start(bf16[2,4,32,576]{3,2,0,1:T(8,128)(2,1)} %pad_maximum_fusion), calls=%async_computation | async-start | bytes 655360 | tf_op jit(solution)/shard_map/all_to_all | solution.py:79
  287.1 6.3 %all-to-all-done = bf16[2,4,32,576]{3,2,0,1:T(8,128)(2,1)S(1)} async-done(((bf16[2,4,32,576]{3,2,0,1:T(8,128)(2,1)}), bf16[2,4,32,576]{3,2,0,1:T(8,128)(2,1)S(1)}, u32[]{:S(2)}, u32[]{:S(2)}) %all-to-all-start) | async-done | bytes 294944 | tf_op jit(solution)/shard_map/all_to_all | solution.py:79
  293.9 0.7 fusion.38
  294.7 0.3 fusion.18
  295.3 0.5 fusion.6
  295.8 1.0 copy.44
  296.7 3.4 %all-to-all-start.1 = ((bf16[2,1,128,512]{3,0,1,2:T(2,128)(2,1)}), bf16[2,1,128,512]{3,0,1,2:T(2,128)(2,1)S(1)}, u32[]{:S(2)}, u32[]{:S(2)}) async-start(bf16[2,1,128,512]{3,0,1,2:T(2,128)(2,1)} %copy.44), calls=%async_computation.1 | async-start | bytes 524288 | tf_op jit(solution)/shard_map/all_to_all | solution.py:81
  300.2 6.5 %copy.46 = bf16[512,4096]{0,1:T(8,128)(2,1)} copy(bf16[512,4096]{1,0:T(8,128)(2,1)} %all-gather.11.cloned.1.call-done) | data formatting | bytes 8388608 | tf_op jit(solution)/shard_map/all_gather | solution.py:60
  306.7 3.4 %fusion.14 = bf16[32,2,1,4,128]{4,3,2,1,0:T(4,128)(2,1)S(1)} fusion(bf16[512,32,128,1]{0,2,3,1:T(8,128)(2,1)} %bitcast.88, bf16[2,4,32,512]{3,0,2,1:T(2,128)(2,1)S(1)} %bitcast.93), kind=kOutput, calls=%fused_computation.13 | convolution fusion | flops 33587200 | bytes 4521984 | tf_op jit(solution)/shard_map/sghc,chv->sghv/dot_general | solution.py:83
  310.1 0.7 copy.65
  (29 shorter events, 1.4 us)
Async XLA Ops:
  6.5 52.0 %all-gather.7.cloned.1.call-start = ((), (), s32[]{:S(2)}) async-start(), calls=%async_computation.3 | async-start | bytes 4718592 | tf_op jit(solution)/shard_map/all_gather | solution.py:59
  7.3 116.5 %all-gather.9.cloned.1.call-start = ((), (), s32[]{:S(2)}) async-start(), calls=%async_computation.4 | async-start | bytes 7077888 | tf_op jit(solution)/shard_map/all_gather | solution.py:61
  8.0 232.8 %all-gather.5.cloned.1.call-start = ((), (), s32[]{:S(2)}) async-start(), calls=%async_computation.2 | async-start | bytes 14155776 | tf_op jit(solution)/shard_map/all_gather | solution.py:64
  8.7 291.4 %all-gather.11.cloned.1.call-start = ((), (), s32[]{:S(2)}) async-start(), calls=%async_computation.5 | async-start | bytes 4718592 | tf_op jit(solution)/shard_map/all_gather | solution.py:60
  282.4 11.3 %copy-start = (bf16[2,1,576]{2,0,1:T(2,128)(2,1)S(1)}, bf16[2,1,576]{2,0,1:T(2,128)(2,1)}, u32[]{:S(2)}) copy-start(bf16[2,1,576]{2,0,1:T(2,128)(2,1)} %param.14) | copy-start | bytes 6916
  282.4 11.5 %copy-start.1 = (bf16[1,1024,576]{1,2,0:T(8,128)(2,1)S(1)}, bf16[1,1024,576]{1,2,0:T(8,128)(2,1)}, u32[]{:S(2)}) copy-start(bf16[1,1024,576]{1,2,0:T(8,128)(2,1)} %param.13) | copy-start | bytes 3538948
  283.4 10.1 %all-to-all-start = ((bf16[2,4,32,576]{3,2,0,1:T(8,128)(2,1)}), bf16[2,4,32,576]{3,2,0,1:T(8,128)(2,1)S(1)}, u32[]{:S(2)}, u32[]{:S(2)}) async-start(bf16[2,4,32,576]{3,2,0,1:T(8,128)(2,1)} %pad_maximum_fusion), calls=%async_computation | async-start | bytes 655360 | tf_op jit(solution)/shard_map/all_to_all | solution.py:79
  296.7 9.9 %all-to-all-start.1 = ((bf16[2,1,128,512]{3,0,1,2:T(2,128)(2,1)}), bf16[2,1,128,512]{3,0,1,2:T(2,128)(2,1)S(1)}, u32[]{:S(2)}, u32[]{:S(2)}) async-start(bf16[2,1,128,512]{3,0,1,2:T(2,128)(2,1)} %copy.44), calls=%async_computation.1 | async-start | bytes 524288 | tf_op jit(solution)/shard_map/all_to_all | solution.py:81
Sparse Core Ops, SparseCore 0:
  8.9 49.5 all-gather.6
  60.2 63.4 all-gather.8
  125.4 115.3 all-gather.4
  242.2 45.0 all-gather.10
where the time goes:
time: 318 us; the launch traced here: 317 us
  waiting for transfers between devices  228 us (72%)
  matrix products  33.7 us (11%)
  local copies, waits for them, and re-layouts  33.4 us (11%)
  between operations  13.9 us (4%)
  starting transfers between devices  7.18 us (2%)
    all_gather x1, waiting for transfers between devices, per_device(): slab = lax.all_gather(w_uq, 'fsdp', axis=0, tiled=True)  113 us
    all_gather x1, waiting for transfers between devices, per_device(): lax.all_gather(w_qr, 'fsdp', axis=0, tiled=True)  58.7 us
    all_gather x1, waiting for transfers between devices, per_device(): lax.all_gather(w_uk, 'fsdp', axis=0, tiled=True)  46.9 us
    dot_general x1, matrix products, per_device(): jnp.einsum('qr,hrc->qhc', flattened, absorbed, preferred_element_type=jnp...  24.9 us
    all_gather x1, local copies, waits for them, and re-layouts, per_device(): slab = lax.all_gather(w_uq, 'fsdp', axis=0, tiled=True)  16.7 us
    all_gather x1, local copies, waits for them, and re-layouts, per_device(): lax.all_gather(w_uk, 'fsdp', axis=0, tiled=True)  6.49 us
    all_gather x1, local copies, waits for them, and re-layouts, per_device(): lax.all_gather(w_uv, 'fsdp', axis=0, tiled=True)  6.48 us
  transfers between devices with their start and end apart: 6, of which 4 were waited for; matrix products, arithmetic and copies ran while one was open for 20% of the time, Pallas kernels for 0%

commit v1 on v0

--- a/solution.py
+++ b/solution.py
@@ -61,7 +61,12 @@
         lax.all_gather(w_qr, "fsdp", axis=0, tiled=True),
     )
     key_heads = key_up.reshape(key_up.shape[0], heads, NOPE)
-    slab = lax.all_gather(w_uq, "fsdp", axis=0, tiled=True)
+    ring = [w_uq]
+    for hop in range(7):
+        ring.append(lax.ppermute(ring[-1], "fsdp", [(dev, (dev + 1) % 8) for dev in range(8)]))
+    slab = jnp.roll(
+        jnp.concatenate(ring[::-1], axis=0), (lax.axis_index("fsdp") + 1) * ring[0].shape[0], axis=0
+    )
     count = slab.shape[0]
     slab_heads = slab.reshape(count, heads, NOPE)
     absorbed = jnp.einsum("rhn,chn->hrc", slab_heads, key_heads, preferred_element_type=jnp.float32)

time: 318 us -> 410 us (1.29)
  the two profiles are of different devices: /device:TPU:0 before, /device:TPU:19 now
where the time goes in v1:
time: 410 us; the launch traced here: 404 us
  waiting for transfers between devices  223 us (54%)
  local copies, waits for them, and re-layouts  107 us (26%)
  matrix products  33.8 us (8%)
  starting transfers between devices  25.3 us (6%)
  between operations  14 us (3%)
    ppermute x7, waiting for transfers between devices, per_device(): lax.ppermute(ring[-1], 'fsdp', [(dev, (dev + 1) % 8) for dev in range(8)])  217 us
    concatenate x1, local copies, waits for them, and re-layouts, per_device(): jnp.roll(jnp.concatenate(ring[::-1], axis=0), (lax.axis_index('fsdp') + 1...  43.7 us
    ppermute x7, local copies, waits for them, and re-layouts, per_device(): lax.ppermute(ring[-1], 'fsdp', [(dev, (dev + 1) % 8) for dev in range(8)])  26.9 us
    dot_general x1, matrix products, per_device(): jnp.einsum('qr,hrc->qhc', flattened, absorbed, preferred_element_type=jnp...  24.9 us
    ppermute x7, starting transfers between devices, per_device(): lax.ppermute(ring[-1], 'fsdp', [(dev, (dev + 1) % 8) for dev in range(8)])  17.9 us
    dynamic_slice x1, local copies, waits for them, and re-layouts, per_device(): jnp.roll(jnp.concatenate(ring[::-1], axis=0), (lax.axis_index('fsdp') + 1...  13 us
  transfers between devices with their start and end apart: 12, of which 7 were waited for; matrix products, arithmetic and copies ran while one was open for 33% of the time, Pallas kernels for 0%

profile of v1, /device:TPU:19, one launch (start us, length us, event | category | flops | bytes accessed | tf_op | source)
XLA Modules:
  0.0 404.0 jit_solution(8012352299098657799)
XLA Ops:
  10.0 51.4 %collective-permute-done = bf16[192,4096]{1,0:T(8,128)(2,1)S(1)} collective-permute-done((bf16[192,4096]{1,0:T(8,128)(2,1)}, bf16[192,4096]{1,0:T(8,128)(2,1)S(1)}, u32[]{:S(2)}, u32[]{:S(2)}) %collective-permute-start) | collective-permute-done | bytes 1572896 | tf_op jit(solution)/shard_map/ppermute | solution.py:66
  64.9 24.6 %collective-permute-done.1 = bf16[192,4096]{1,0:T(8,128)(2,1)S(1)} collective-permute-done((bf16[192,4096]{1,0:T(8,128)(2,1)S(1)}, bf16[192,4096]{1,0:T(8,128)(2,1)S(1)}, u32[]{:S(2)}, u32[]{:S(2)}) %collective-permute-start.1) | collective-permute-done | bytes 1572896 | tf_op jit(solution)/shard_map/ppermute | solution.py:66
  90.6 3.5 collective-permute-start.2
  94.1 55.5 %collective-permute-done.2 = bf16[192,4096]{1,0:T(8,128)(2,1)S(1)} collective-permute-done((bf16[192,4096]{1,0:T(8,128)(2,1)S(1)}, bf16[192,4096]{1,0:T(8,128)(2,1)S(1)}, u32[]{:S(2)}, u32[]{:S(2)}) %collective-permute-start.2) | collective-permute-done | bytes 1572896 | tf_op jit(solution)/shard_map/ppermute | solution.py:66
  153.2 17.4 %collective-permute-done.3 = bf16[192,4096]{1,0:T(8,128)(2,1)S(1)} collective-permute-done((bf16[192,4096]{1,0:T(8,128)(2,1)S(1)}, bf16[192,4096]{1,0:T(8,128)(2,1)S(1)}, u32[]{:S(2)}, u32[]{:S(2)}) %collective-permute-start.3) | collective-permute-done | bytes 1572896 | tf_op jit(solution)/shard_map/ppermute | solution.py:66
  174.2 17.4 %collective-permute-done.4 = bf16[192,4096]{1,0:T(8,128)(2,1)S(1)} collective-permute-done((bf16[192,4096]{1,0:T(8,128)(2,1)S(1)}, bf16[192,4096]{1,0:T(8,128)(2,1)S(1)}, u32[]{:S(2)}, u32[]{:S(2)}) %collective-permute-start.4) | collective-permute-done | bytes 1572896 | tf_op jit(solution)/shard_map/ppermute | solution.py:66
  194.1 51.0 %collective-permute-done.5 = bf16[192,4096]{1,0:T(8,128)(2,1)} collective-permute-done((bf16[192,4096]{1,0:T(8,128)(2,1)S(1)}, bf16[192,4096]{1,0:T(8,128)(2,1)}, u32[]{:S(2)}, u32[]{:S(2)}) %collective-permute-start.5) | collective-permute-done | bytes 1572896 | tf_op jit(solution)/shard_map/ppermute | solution.py:66
  251.8 3.9 copy.45
  255.6 3.8 copy.44
  259.5 3.8 copy.43
  263.3 3.8 copy.42
  267.2 6.5 %copy.55 = bf16[512,4096]{0,1:T(8,128)(2,1)} copy(bf16[512,4096]{1,0:T(8,128)(2,1)} %all-gather.4.cloned.1.call-done) | data formatting | bytes 8388608 | tf_op jit(solution)/shard_map/all_gather | solution.py:59
  273.6 3.8 copy.41
  277.5 3.8 copy.40
  281.3 3.8 copy.39
  285.1 43.7 %concatenate.36 = bf16[3072,4096]{0,1:T(8,128)(2,1)} concatenate(bf16[192,4096]{0,1:T(8,128)(2,1)} %copy.39, bf16[192,4096]{0,1:T(8,128)(2,1)} %copy.40, bf16[192,4096]{0,1:T(8,128)(2,1)} %copy.41, bf16[192,4096]{0,1:T(8,128)(2,1)} %copy.42, bf16[192,4096]{0,1:T(8,128)(2,1)} %copy.43, bf16[192,4096]{0,1:T(8,128)(2,1)} %copy.44, bf16[192,4096]{0,1:T(8,128)(2,1)} %copy.45, ...), dimensions={0} | concatenate | bytes 50331648 | tf_op jit(solution)/shard_map/jit(_roll_dynamic)/concatenate | solution.py:67
  328.9 13.0 %constant_dynamic-slice_fusion = bf16[1536,4096]{0,1:T(8,128)(2,1)} fusion(bf16[3072,4096]{0,1:T(8,128)(2,1)} %concatenate.36, s32[]{:T(128)S(6)} %select_n.24), kind=kLoop, calls=%fused_computation.50 | loop fusion | bytes 25165828 | tf_op jit(solution)/shard_map/jit(_roll_dynamic)/dynamic_slice | solution.py:67
  341.9 24.9 %fusion.11 = bf16[8,32,512]{2,0,1:T(8,128)(2,1)S(1)} fusion(bf16[8,1536,1]{1,0,2:T(8,128)(2,1)S(1)} %reshape.301, bf16[1536,32,128]{0,2,1:T(8,128)(2,1)} %bitcast.89, bf16[512,32,128]{0,2,1:T(8,128)(2,1)} %bitcast.90), kind=kOutput, calls=%fused_computation.11 | convolution fusion | flops 6870401024 | bytes 17063936 | tf_op jit(solution)/shard_map/qr,hrc->qhc/dot_general | solution.py:74
  367.0 3.8 convolution_convert_fusion
  371.7 3.7 all-to-all-start
  375.5 4.4 %all-to-all-done = bf16[2,4,32,576]{3,2,0,1:T(8,128)(2,1)S(1)} async-done(((bf16[2,4,32,576]{3,2,0,1:T(8,128)(2,1)}), bf16[2,4,32,576]{3,2,0,1:T(8,128)(2,1)S(1)}, u32[]{:S(2)}, u32[]{:S(2)}) %all-to-all-start) | async-done | bytes 294944 | tf_op jit(solution)/shard_map/all_to_all | solution.py:84
  383.3 3.7 all-to-all-start.1
  387.0 6.5 %copy.63 = bf16[512,4096]{0,1:T(8,128)(2,1)} copy(bf16[512,4096]{1,0:T(8,128)(2,1)} %all-gather.8.cloned.1.call-done) | data formatting | bytes 8388608 | tf_op jit(solution)/shard_map/all_gather | solution.py:60
  393.4 3.4 fusion.14
  (61 shorter events, 28.8 us)
Async XLA Ops:
  6.5 244.4 %copy-start.5 = (bf16[2,4,1536]{2,1,0:T(4,128)(2,1)S(1)}, bf16[2,4,1536]{2,1,0:T(4,128)(2,1)}, u32[]{:S(2)}) copy-start(bf16[2,4,1536]{2,1,0:T(4,128)(2,1)} %param.8) | copy-start | bytes 73732
  6.5 260.6 %all-gather.4.cloned.1.call-start = ((), (), s32[]{:S(2)}) async-start(), calls=%async_computation.2 | async-start | bytes 4718592 | tf_op jit(solution)/shard_map/all_gather | solution.py:59
  7.3 359.8 %all-gather.6.cloned.1.call-start = ((), (), s32[]{:S(2)}) async-start(), calls=%async_computation.3 | async-start | bytes 7077888 | tf_op jit(solution)/shard_map/all_gather | solution.py:61
  8.0 378.9 %all-gather.8.cloned.1.call-start = ((), (), s32[]{:S(2)}) async-start(), calls=%async_computation.4 | async-start | bytes 4718592 | tf_op jit(solution)/shard_map/all_gather | solution.py:60
  8.1 53.3 %collective-permute-start = (bf16[192,4096]{1,0:T(8,128)(2,1)}, bf16[192,4096]{1,0:T(8,128)(2,1)S(1)}, u32[]{:S(2)}, u32[]{:S(2)}) collective-permute-start(bf16[192,4096]{1,0:T(8,128)(2,1)} %param.9), channel_id=1, source_target_pairs={{0,4},{4,8},{8,12},{12,16},{16,20},{20,24},{24,28},{28,0},{1,5},{5... | collective-permute-start | bytes 4718600 | tf_op jit(solution)/shard_map/ppermute | solution.py:66
  61.3 1.1 copy-start
  62.5 26.9 %collective-permute-start.1 = (bf16[192,4096]{1,0:T(8,128)(2,1)S(1)}, bf16[192,4096]{1,0:T(8,128)(2,1)S(1)}, u32[]{:S(2)}, u32[]{:S(2)}) collective-permute-start(bf16[192,4096]{1,0:T(8,128)(2,1)S(1)} %collective-permute-done), channel_id=1, source_target_pairs={{0,4},{4,8},{8,12},{12,16},{16,20},{20,24},{24,28},{28,0},{1,5},{5... | collective-permute-start | bytes 4718600 | tf_op jit(solution)/shard_map/ppermute | solution.py:66
  89.4 1.2 copy-start.1
  90.6 59.0 %collective-permute-start.2 = (bf16[192,4096]{1,0:T(8,128)(2,1)S(1)}, bf16[192,4096]{1,0:T(8,128)(2,1)S(1)}, u32[]{:S(2)}, u32[]{:S(2)}) collective-permute-start(bf16[192,4096]{1,0:T(8,128)(2,1)S(1)} %collective-permute-done.1), channel_id=1, source_target_pairs={{0,4},{4,8},{8,12},{12,16},{16,20},{20,24},{24,28},{28,0},{1,5},{5... | collective-permute-start | bytes 4718600 | tf_op jit(solution)/shard_map/ppermute | solution.py:66
  149.6 1.1 copy-start.2
  150.8 19.8 %collective-permute-start.3 = (bf16[192,4096]{1,0:T(8,128)(2,1)S(1)}, bf16[192,4096]{1,0:T(8,128)(2,1)S(1)}, u32[]{:S(2)}, u32[]{:S(2)}) collective-permute-start(bf16[192,4096]{1,0:T(8,128)(2,1)S(1)} %collective-permute-done.2), channel_id=1, source_target_pairs={{0,4},{4,8},{8,12},{12,16},{16,20},{20,24},{24,28},{28,0},{1,5},{5... | collective-permute-start | bytes 4718600 | tf_op jit(solution)/shard_map/ppermute | solution.py:66
  170.6 1.1 copy-start.3
  171.8 19.8 %collective-permute-start.4 = (bf16[192,4096]{1,0:T(8,128)(2,1)S(1)}, bf16[192,4096]{1,0:T(8,128)(2,1)S(1)}, u32[]{:S(2)}, u32[]{:S(2)}) collective-permute-start(bf16[192,4096]{1,0:T(8,128)(2,1)S(1)} %collective-permute-done.3), channel_id=1, source_target_pairs={{0,4},{4,8},{8,12},{12,16},{16,20},{20,24},{24,28},{28,0},{1,5},{5... | collective-permute-start | bytes 4718600 | tf_op jit(solution)/shard_map/ppermute | solution.py:66
  191.6 56.1 %copy-start.4 = (bf16[192,4096]{1,0:T(8,128)(2,1)}, bf16[192,4096]{1,0:T(8,128)(2,1)S(1)}, u32[]{:S(2)}) copy-start(bf16[192,4096]{1,0:T(8,128)(2,1)S(1)} %collective-permute-done.4) | copy-start | bytes 4718596
  191.6 53.5 %collective-permute-start.5 = (bf16[192,4096]{1,0:T(8,128)(2,1)S(1)}, bf16[192,4096]{1,0:T(8,128)(2,1)}, u32[]{:S(2)}, u32[]{:S(2)}) collective-permute-start(bf16[192,4096]{1,0:T(8,128)(2,1)S(1)} %collective-permute-done.4), channel_id=1, source_target_pairs={{0,4},{4,8},{8,12},{12,16},{16,20},{20,24},{24,28},{28,0},{1,5},{5... | collective-permute-start | bytes 4718600 | tf_op jit(solution)/shard_map/ppermute | solution.py:66
  245.2 36.1 %collective-permute-start.6 = (bf16[192,4096]{1,0:T(8,128)(2,1)}, bf16[192,4096]{1,0:T(8,128)(2,1)}, u32[]{:S(2)}, u32[]{:S(2)}) collective-permute-start(bf16[192,4096]{1,0:T(8,128)(2,1)} %collective-permute-done.5), channel_id=1, source_target_pairs={{0,4},{4,8},{8,12},{12,16},{16,20},{20,24},{24,28},{28,0},{1,5},{5... | collective-permute-start | bytes 4718600 | tf_op jit(solution)/shard_map/ppermute | solution.py:66
  367.0 13.2 %copy-start.6 = (bf16[2,1,576]{2,0,1:T(2,128)(2,1)S(1)}, bf16[2,1,576]{2,0,1:T(2,128)(2,1)}, u32[]{:S(2)}) copy-start(bf16[2,1,576]{2,0,1:T(2,128)(2,1)} %param.14) | copy-start | bytes 6916
  367.0 13.4 %copy-start.7 = (bf16[1,1024,576]{1,2,0:T(8,128)(2,1)S(1)}, bf16[1,1024,576]{1,2,0:T(8,128)(2,1)}, u32[]{:S(2)}) copy-start(bf16[1,1024,576]{1,2,0:T(8,128)(2,1)} %param.13) | copy-start | bytes 3538948
  371.7 8.2 %all-to-all-start = ((bf16[2,4,32,576]{3,2,0,1:T(8,128)(2,1)}), bf16[2,4,32,576]{3,2,0,1:T(8,128)(2,1)S(1)}, u32[]{:S(2)}, u32[]{:S(2)}) async-start(bf16[2,4,32,576]{3,2,0,1:T(8,128)(2,1)} %pad_maximum_fusion), calls=%async_computation | async-start | bytes 655360 | tf_op jit(solution)/shard_map/all_to_all | solution.py:84
  383.3 10.1 %all-to-all-start.1 = ((bf16[2,1,128,512]{3,0,1,2:T(2,128)(2,1)}), bf16[2,1,128,512]{3,0,1,2:T(2,128)(2,1)S(1)}, u32[]{:S(2)}, u32[]{:S(2)}) async-start(bf16[2,1,128,512]{3,0,1,2:T(2,128)(2,1)} %copy.61), calls=%async_computation.1 | async-start | bytes 524288 | tf_op jit(solution)/shard_map/all_to_all | solution.py:86
Sparse Core Ops, SparseCore 0:
  8.9 61.2 all-gather.3
  71.9 84.0 all-gather.5
  194.2 60.1 all-gather.7
